TPU v7x, 256 devices: a 2x2x32 block of a 4x8x32 slice. The times are simulated.
256 devices in a mesh: groups: 4 (over x, y), blk: 64 (over z, core).
Axes of the slice: x: 2, y: 2, z: 32, core: 2. Of those that a mesh axis runs over, the one named last changes fastest.
The devices are a block of a 4x8x32 slice.
Arguments:
- queries: bfloat16 [128, 64, 2048], P('blk', 'groups'), parts along dimension 1, may hold values from -24 to 24
- keys: bfloat16 [524288, 512], P(('groups', 'blk')), parts along dimension 0, may hold values from -24 to 24
- values: bfloat16 [524288, 512], P(('groups', 'blk')), parts along dimension 0, may hold values from -24 to 24
- out_weight: bfloat16 [2048, 2048], replicated, may hold values from -0.125 to 0.125
- chosen: int32 [64, 12], P('groups'), parts along dimension 0, may hold values from 0 to 255, as said below
- tile_start: int32 [64], P('groups'), parts along dimension 0, may hold values from 0 to 130944, as said below
Outputs:
- projected: bfloat16 [128, 64, 2048], P('blk', 'groups'), parts along dimension 1
There are 4 independent parts, one for each index of `groups`. A program takes and returns all parts, laid end to end along the dimension named above; an argument that names none is the same for every part. Nothing has to cross between parts.
Inputs may be any that keep to these rules, and one draw needn't show every extreme that they name: `chosen`: row t lists 12 different blocks; the first is the block that holds tile t's positions, the others lie before it. Each block is listed by at most 2 tiles, and some block by exactly 2. `tile_start[t]` is a multiple of 128; tile t's queries have positions tile_start[t] to tile_start[t] + 127, all inside block chosen[t, 0].
All inputs are finite; a program needn't handle non-finite values.
Results may differ from a plain program's by a relative error of at most 0.0064.
Values may be sent and summed in bfloat16 or wider, within the bound.
A program may use at most 128 MiB of HBM per device.

v0:
```python
import math

import jax
import jax.numpy as jnp
from jax import lax
from jax.sharding import PartitionSpec as P

QH = 16
KVH = 4
HD = 128
BLOCK = 512
CAP = 2


neg_big = -1e30


def visit_block(query_tile, tile_begin, block_keys, block_values, block_begin):
    tile_rows = query_tile.shape[0]
    key_count = block_keys.shape[0]
    query_view = query_tile.reshape(tile_rows, KVH, QH // KVH, HD)
    key_view = block_keys.reshape(key_count, KVH, HD)
    value_view = block_values.reshape(key_count, KVH, HD)
    scores = jnp.einsum(
        "rkgd,jkd->kgrj", query_view, key_view, preferred_element_type=jnp.float32
    ) * (1.0 / math.sqrt(HD))
    query_pos = tile_begin + jnp.arange(tile_rows, dtype=jnp.int32)
    key_pos = block_begin + jnp.arange(key_count, dtype=jnp.int32)
    visible = key_pos[None, :] <= query_pos[:, None]
    masked = jnp.where(visible, scores, neg_big)
    highest = jnp.max(masked, axis=3, keepdims=True)
    summed = jnp.sum(jnp.where(visible, jnp.exp(masked - highest), 0.0), axis=3, keepdims=True)
    log_total = highest + jnp.log(summed)
    weights = jnp.where(visible, jnp.exp(masked - log_total), 0.0).astype(jnp.bfloat16)
    partial_value = jnp.einsum(
        "kgrj,jkd->rkgd", weights, value_view, preferred_element_type=jnp.float32
    )
    partial_value = partial_value.astype(jnp.bfloat16).reshape(tile_rows, QH * HD)
    log_rows = jnp.transpose(log_total[..., 0], (2, 0, 1)).reshape(tile_rows, QH)
    return (partial_value, log_rows)


def slot_table(chosen, block_count):
    tile_count = chosen.shape[0]
    block_ids = jnp.arange(block_count, dtype=jnp.int32)
    tile_index = jnp.arange(tile_count, dtype=jnp.int32)
    member = jnp.any(chosen[None, :, :] == block_ids[:, None, None], axis=2)
    ranking = jnp.cumsum(member.astype(jnp.int32), axis=1) - 1
    slot_index = jnp.arange(CAP, dtype=jnp.int32)
    hits = member[:, None, :] & (ranking[:, None, :] == slot_index[None, :, None])
    slot_tile = jnp.sum(jnp.where(hits, tile_index[None, None, :], 0), axis=2)
    slot_live = jnp.any(hits, axis=2)
    return (hits, slot_tile, slot_live)


def on_device(queries, keys, values, out_weight, chosen, tile_start):
    owner_count = lax.axis_size("blk")
    owner_dev = lax.axis_index("blk")
    local_rows, tile_count, width = queries.shape
    per_device = keys.shape[0] // BLOCK
    slot_count = per_device * CAP
    head_count = QH
    hits_blocks, tiles_blocks, live_blocks = slot_table(chosen, owner_count * per_device)
    tiles_all = tiles_blocks.reshape(owner_count, slot_count)
    live_all = live_blocks.reshape(owner_count, slot_count)
    my_tiles = tiles_all[owner_dev]
    my_live = live_all[owner_dev]
    begins = tile_start[my_tiles]
    local_block = jnp.arange(slot_count, dtype=jnp.int32) // CAP
    gathered = lax.all_gather(queries, "blk", axis=0, tiled=True)
    slot_queries = jnp.transpose(jnp.take(gathered, my_tiles, axis=1), (1, 0, 2))

    def one_slot(inputs):
        query_tile, tile_begin, block_here = inputs
        offset = block_here * BLOCK
        block_keys = lax.dynamic_slice_in_dim(keys, offset, BLOCK, 0)
        block_values = lax.dynamic_slice_in_dim(values, offset, BLOCK, 0)
        block_begin = (owner_dev * per_device + block_here) * BLOCK
        return visit_block(query_tile, tile_begin, block_keys, block_values, block_begin)

    partials, log_slots = lax.map(one_slot, (slot_queries, begins, local_block))
    log_slots = jnp.where(my_live[:, None, None], log_slots, neg_big)
    part_out = partials.reshape(slot_count, owner_count, local_rows, width)
    peak_out = log_slots.reshape(slot_count, owner_count, local_rows, head_count)
    got_parts = lax.all_to_all(part_out, "blk", split_axis=1, concat_axis=1, tiled=True)
    got_peaks = lax.all_to_all(peak_out, "blk", split_axis=1, concat_axis=1, tiled=True)
    pair_count = slot_count * owner_count
    pair_tile = jnp.transpose(tiles_all).reshape(pair_count)
    pair_live = jnp.transpose(live_all).reshape(pair_count)
    tile_index = jnp.arange(tile_count, dtype=jnp.int32)
    pair_hits = (pair_tile[None, :] == tile_index[:, None]) & pair_live[None, :]
    peaks = got_peaks.reshape(pair_count, local_rows, head_count)
    tile_peak = jnp.max(jnp.where(pair_hits[:, :, None, None], peaks[None], neg_big), axis=1)
    pair_peak = tile_peak[pair_tile]
    factor = jnp.where(pair_live[:, None, None], jnp.exp(peaks - pair_peak), 0.0)
    weighted = factor[..., None] * got_parts.reshape(pair_count, local_rows, head_count, -1).astype(
        jnp.float32
    )
    weighted = weighted.reshape(pair_count, local_rows, width)
    pick_table = pair_hits.astype(jnp.float32)
    numer_rows = jnp.einsum("tp,prf->rtf", pick_table, weighted, precision=lax.Precision.HIGHEST)
    denom_rows = jnp.einsum("tp,prh->rth", pick_table, factor, precision=lax.Precision.HIGHEST)
    merged = numer_rows.reshape(local_rows, tile_count, head_count, -1) / denom_rows[..., None]
    merged = merged.reshape(local_rows * tile_count, width).astype(jnp.bfloat16)
    result = jnp.dot(merged, out_weight, preferred_element_type=jnp.float32).astype(jnp.bfloat16)
    return result.reshape(local_rows, tile_count, out_weight.shape[1])


def solution(mesh):
    placed = (
        P("blk", "groups", None),
        P(("groups", "blk"), None),
        P(("groups", "blk"), None),
        P(),
        P("groups", None),
        P("groups"),
    )
    return jax.shard_map(
        on_device, mesh=mesh, in_specs=placed, out_specs=P("blk", "groups", None), check_vma=False
    )
```

profile of v0, /device:TPU:46, one launch (start us, length us, event | category | flops | bytes accessed | tf_op | source)
XLA Modules:
  0.0 728.1 jit_solution(17762847718979088911)
XLA Ops:
  9.6 149.6 %all-gather.2.cloned.1.call-done = bf16[128,16,2048]{2,1,0:T(8,128)(2,1)} async-done(((bf16[2,16,2048]{2,1,0:T(8,128)(2,1)}), bf16[128,16,2048]{2,1,0:T(8,128)(2,1)}) %all-gather.2.cloned.1.call-update) | async-done | bytes 8388624 | tf_op jit(solution)/shard_map/all_gather | solution.py:70
  159.2 11.2 %copy.79 = bf16[128,16,2048]{2,0,1:T(8,128)(2,1)} copy(bf16[128,16,2048]{2,1,0:T(8,128)(2,1)} %all-gather.2.cloned.1.call-done) | data formatting | bytes 16777216 | tf_op jit(solution)/shard_map/all_gather | solution.py:70
  170.4 6.1 gather_fusion.1
  176.6 4.6 broadcast_select_fusion
  181.1 81.9 %while.14 = (s32[]{:T(128)}, bf16[8,128,2048]{1,2,0:T(8,128)(2,1)}, f32[8,128,16]{1,2,0:T(8,128)S(1)}, s32[8]{0:T(128)S(1)}, bf16[2048,512]{1,0:T(8,128)(2,1)}, ...) while((s32[]{:T(128)}, bf16[8,128,2048]{1,2,0:T(8,128)(2,1)}, ...), condition=%wide.region_7.8_spmd, body=%wide.region_4.7_spmd.sunk | while | flops 550828672 | bytes 22361340 | solution.py:81
  182.3 1.3 constant_dynamic-slice_fusion.6
  192.6 1.3 constant_dynamic-slice_fusion.6
  202.8 1.3 constant_dynamic-slice_fusion.6
  213.1 1.3 constant_dynamic-slice_fusion.6
  223.3 1.3 constant_dynamic-slice_fusion.6
  243.8 1.3 constant_dynamic-slice_fusion.6
  264.2 14.5 %all-to-all-start = ((f32[64,1,256]{2,1,0:T(1,128)}), f32[64,1,256]{2,1,0:T(1,128)S(1)}, u32[]{:S(2)}, u32[]{:S(2)}) async-start(f32[64,1,256]{2,1,0:T(1,128)} %reshape.230), calls=%async_computation | async-start | bytes 131072 | tf_op jit(solution)/shard_map/all_to_all | solution.py:86
  278.7 6.7 copy.89
  285.4 18.1 %all-to-all-done = f32[64,1,256]{2,1,0:T(1,128)S(1)} async-done(((f32[64,1,256]{2,1,0:T(1,128)}), f32[64,1,256]{2,1,0:T(1,128)S(1)}, u32[]{:S(2)}, u32[]{:S(2)}) %all-to-all-start) | async-done | bytes 65568 | tf_op jit(solution)/shard_map/all_to_all | solution.py:86
  303.5 7.3 %all-to-all-start.1 = ((bf16[8,64,2,2048]{3,0,2,1:T(8,128)(2,1)}), bf16[8,64,2,2048]{3,0,2,1:T(8,128)(2,1)}, u32[]{:S(2)}, u32[]{:S(2)}) async-start(bf16[8,64,2,2048]{3,0,2,1:T(8,128)(2,1)} %bitcast.114), calls=%async_computation.1 | async-start | bytes 8388608 | tf_op jit(solution)/shard_map/all_to_all | solution.py:85
  313.4 2.1 gather_fusion.2
  315.5 1.8 exponential_select_fusion
  318.0 5.1 mul.35
  323.1 9.3 %mul.36 = f32[512,2,2048]{2,0,1:T(8,128)} reshape(f32[512,2,16,128]{3,2,0,1:T(8,128)} %mul.35) | data formatting | bytes 16777216 | tf_op jit(solution)/shard_map/mul | solution.py:96
  332.4 357.4 %all-to-all-done.1 = bf16[8,64,2,2048]{3,0,2,1:T(8,128)(2,1)} async-done(((bf16[8,64,2,2048]{3,0,2,1:T(8,128)(2,1)}), bf16[8,64,2,2048]{3,0,2,1:T(8,128)(2,1)}, u32[]{:S(2)}, u32[]{:S(2)}) %all-to-all-start.1) | async-done | bytes 4194336 | tf_op jit(solution)/shard_map/all_to_all | solution.py:85
  689.8 7.8 %copy.90 = f32[8,64,2,2048]{3,1,0,2:T(8,128)} copy(bf16[8,64,2,2048]{3,0,2,1:T(8,128)(2,1)} %all-to-all-done.1) | data formatting | bytes 12582912 | tf_op jit(solution)/shard_map/convert_element_type | solution.py:96
  697.6 11.7 %bitcast_multiply_fusion = f32[512,2,2048]{2,0,1:T(8,128)} fusion(f32[512,2,2048]{2,0,1:T(8,128)} %mul.36, f32[8,64,2,2048]{3,1,0,2:T(8,128)} %copy.90), kind=kLoop, calls=%fused_computation.22 | loop fusion | flops 2097152 | bytes 25165824 | tf_op jit(solution)/shard_map/mul | solution.py:96
  709.3 6.1 fusion.13
  715.7 5.6 convolution_convert_fusion
  (169 shorter events, 71.4 us)
Async XLA Ops:
  6.5 2.4 copy-start
  6.6 152.7 %all-gather.2.cloned.1.call-start = ((), (), s32[]{:S(2)}) async-start(), calls=%async_computation.2 | async-start | bytes 8519680 | tf_op jit(solution)/shard_map/all_gather | solution.py:70
  264.2 39.4 %all-to-all-start = ((f32[64,1,256]{2,1,0:T(1,128)}), f32[64,1,256]{2,1,0:T(1,128)S(1)}, u32[]{:S(2)}, u32[]{:S(2)}) async-start(f32[64,1,256]{2,1,0:T(1,128)} %reshape.230), calls=%async_computation | async-start | bytes 131072 | tf_op jit(solution)/shard_map/all_to_all | solution.py:86
  303.5 386.3 %all-to-all-start.1 = ((bf16[8,64,2,2048]{3,0,2,1:T(8,128)(2,1)}), bf16[8,64,2,2048]{3,0,2,1:T(8,128)(2,1)}, u32[]{:S(2)}, u32[]{:S(2)}) async-start(bf16[8,64,2,2048]{3,0,2,1:T(8,128)(2,1)} %bitcast.114), calls=%async_computation.1 | async-start | bytes 8388608 | tf_op jit(solution)/shard_map/all_to_all | solution.py:85
  715.6 5.7 copy-start.1
Sparse Core Ops, SparseCore 0:
  9.2 149.9 all-gather.1
where the time goes:
time: 730 us; the launch traced here: 728 us
  waiting for transfers between devices  526 us (72%)
  local copies, waits for them, and re-layouts  94.1 us (13%)
  other arithmetic  33.9 us (5%)
  matrix products  28.4 us (4%)
  starting transfers between devices  21.8 us (3%)
  between operations  13.6 us (2%)
  loops' own time  10.4 us (1%)
    all_to_all x1, waiting for transfers between devices, on_device(): lax.all_to_all(part_out, 'blk', split_axis=1, concat_axis=1, tiled=True)  357 us
    all_gather x1, waiting for transfers between devices, on_device(): gathered = lax.all_gather(queries, 'blk', axis=0, tiled=True)  150 us
    dynamic_slice x32, local copies, waits for them, and re-layouts, on_device(): partials, log_slots = lax.map(one_slot, (slot_queries, begins, local_block))  20.5 us
    all_to_all x1, waiting for transfers between devices, on_device(): lax.all_to_all(peak_out, 'blk', split_axis=1, concat_axis=1, tiled=True)  18.1 us
  transfers between devices with their start and end apart: 3, of which 3 were waited for; matrix products, arithmetic and copies ran while one was open for 4% of the time, Pallas kernels for 0%

commit v1 on v0

v1 whole, which is shorter than its diff:
```python
import functools
import math

import jax
import jax.numpy as jnp
from jax import lax
from jax.experimental import pallas as pl
from jax.experimental.pallas import tpu as pltpu
from jax.sharding import PartitionSpec as P

QH = 16
KVH = 4
GRP = QH // KVH
HD = 128
BLOCK = 512
CAP = 2
PIECES = 2
TERMS = 3
CHUNK_ROWS = 128
VMEM_LIMIT = 60 * 1024 * 1024

MESH = pl.DeviceIdType.MESH
neg_big = -1e30


class Ring:
    def __init__(self, n_dev, cores):
        self.cores = cores
        self.chips = n_dev // cores
        self.ups = self.chips // 2
        self.dns = self.chips - 1 - self.ups
        me = lax.axis_index("blk")
        self.me, self.z, self.core = me, me // cores, me % cores
        self.partner = self.z * cores + (1 - self.core)
        self.above = ((self.z + 1) % self.chips) * cores + self.core
        self.below = ((self.z + self.chips - 1) % self.chips) * cores + self.core

    def greet(self):
        barrier = pltpu.get_barrier_semaphore()
        for target in (self.above, self.below, self.partner):
            pl.semaphore_signal(barrier, inc=1, device_id={"blk": target}, device_id_type=MESH)
        pl.semaphore_wait(barrier, 3)


def remote(src, dst, send_sem, recv_sem, target):
    return pltpu.make_async_remote_copy(
        src_ref=src,
        dst_ref=dst,
        send_sem=send_sem,
        recv_sem=recv_sem,
        device_id={"blk": target},
        device_id_type=MESH,
    )


def send(src, dst, send_sem, recv_sem, target):
    remote(src, dst, send_sem, recv_sem, target).start()


def gather_kernel(
    cores,
    per_device,
    chosen_ref,
    q_hbm,
    all_hbm,
    slot_tab,
    last_tab,
    gath,
    own_sem,
    store_sem,
    ag_up_out,
    ag_up,
    ag_dn_out,
    ag_dn,
    ag_pt_out,
    ag_pt,
):
    n_dev, tiles, _, sub, _ = gath.shape
    slots = per_device * CAP
    group = tiles // PIECES
    topk = chosen_ref.shape[1]
    ring = Ring(n_dev, cores)
    chips, ups, dns, cores = ring.chips, ring.ups, ring.dns, ring.cores
    me, z, core = ring.me, ring.z, ring.core
    above, below, partner = ring.above, ring.below, ring.partner

    def drain(ref, sem):
        remote(ref, ref, sem, sem, partner).wait_recv()

    def gone(ref, sem):
        remote(ref, ref, sem, sem, partner).wait_send()

    own_load = pltpu.make_async_copy(q_hbm, gath.at[me], own_sem)
    own_load.start()
    ring.greet()
    own_load.wait()

    def shard(index, piece):
        return gath.at[index, pl.ds(piece * group, group)]

    def to_partner(index):
        part = gath.at[index]
        send(part, part, ag_pt_out.at[index // cores], ag_pt.at[index // cores], partner)

    def gather_step(step, carry):
        from_below = ((z - step + chips) % chips) * cores + core
        from_above = ((z + step) % chips) * cores + core
        for piece in range(PIECES):
            part = shard(from_below, piece)

            @pl.when(step >= 1)
            def _():
                drain(part, ag_up.at[step - 1, piece])

            send(part, part, ag_up_out.at[step, piece], ag_up.at[step, piece], above)

            @pl.when(step < dns)
            def _():
                other = shard(from_above, piece)

                @pl.when(step >= 1)
                def _():
                    drain(other, ag_dn.at[step - 1, piece])

                send(other, other, ag_dn_out.at[step, piece], ag_dn.at[step, piece], below)

        to_partner(from_below)

        @pl.when((step >= 1) & (step < dns))
        def _():
            to_partner(from_above)

        return carry

    lax.fori_loop(0, ups, gather_step, 0)

    def scan_tile(tile, carry):
        firsts, lasts = carry
        new_firsts, new_lasts = [], []
        for block in range(per_device):
            hit = chosen_ref[tile, 0] == me * per_device + block
            for pick in range(1, topk):
                hit = hit | (chosen_ref[tile, pick] == me * per_device + block)
            fresh = hit & (firsts[block] == tiles)
            new_firsts.append(jnp.where(fresh, tile, firsts[block]))
            new_lasts.append(jnp.where(hit, tile, lasts[block]))
        return tuple(new_firsts), tuple(new_lasts)

    none_yet = (jnp.int32(tiles),) * per_device, (jnp.int32(-1),) * per_device
    firsts, lasts = lax.fori_loop(0, tiles, scan_tile, none_yet)
    slot_tile, slot_live = [], []
    for block in range(per_device):
        live = firsts[block] < tiles
        twice = lasts[block] > firsts[block]
        slot_tile += [jnp.where(live, firsts[block], 0), jnp.where(twice, lasts[block], 0)]
        slot_live += [live, twice]
    for slot in range(slots):
        previous = jnp.int32(slots)
        for before in range(slot):
            same = slot_live[before] & slot_live[slot] & (slot_tile[before] == slot_tile[slot])
            previous = jnp.where(same, before, previous)
        slot_tab[0, slot] = slot_tile[slot]
        slot_tab[1, slot] = jnp.where(slot_live[slot], 1, 0)
        slot_tab[2, slot] = previous
    for tile in range(tiles):
        latest = jnp.int32(slots)
        for slot in range(slots):
            latest = jnp.where(slot_live[slot] & (slot_tile[slot] == tile), slot, latest)
        last_tab[tile] = latest

    from_below = ((z - ups + chips) % chips) * cores + core
    from_above = ((z + dns) % chips) * cores + core
    for piece in range(PIECES):
        drain(shard(from_below, piece), ag_up.at[ups - 1, piece])
    to_partner(from_below)
    for piece in range(PIECES):
        drain(shard(from_above, piece), ag_dn.at[dns - 1, piece])
    to_partner(from_above)

    def partner_shard(chip, carry):
        drain(gath.at[chip * cores + (1 - core)], ag_pt.at[chip])
        for index in (chip * cores + core, chip * cores + (1 - core)):
            pltpu.make_async_copy(gath.at[index], all_hbm.at[index], store_sem.at[index]).start()
        return carry

    lax.fori_loop(0, chips, partner_shard, 0)
    def left(step, carry):
        for piece in range(PIECES):
            gone(shard(((z - step + chips) % chips) * cores + core, piece), ag_up_out.at[step, piece])

            @pl.when(step < dns)
            def _():
                gone(shard(((z + step) % chips) * cores + core, piece), ag_dn_out.at[step, piece])

        return carry

    lax.fori_loop(0, ups, left, 0)

    def left_partner(chip, carry):
        gone(gath.at[chip * cores + core], ag_pt_out.at[chip])
        return carry

    lax.fori_loop(0, chips, left_partner, 0)

    def stored(index, carry):
        pltpu.make_async_copy(gath.at[index], all_hbm.at[index], store_sem.at[index]).wait()
        return carry

    lax.fori_loop(0, n_dev, stored, 0)


def visit_kernel(slot_tab, start_ref, q_ref, k_ref, v_ref, acc, accl):
    slot = pl.program_id(0)
    slots = pl.num_programs(0)
    n_dev, _, _, sub, _ = q_ref.shape
    rows = n_dev * sub
    chunk_rows = min(CHUNK_ROWS, rows)
    chunk_devs = chunk_rows // sub
    chunks = rows // chunk_rows
    per_device = slots // CAP
    block = slot // CAP
    tile = slot_tab[0, slot]
    previous = slot_tab[2, slot]
    offset = start_ref[tile] - (lax.axis_index("blk") * per_device + block) * BLOCK

    @pl.when(slot == 0)
    def _():
        acc[slots] = jnp.zeros(acc.shape[1:], acc.dtype)
        accl[slots] = jnp.full(accl.shape[1:], neg_big, accl.dtype)

    @pl.when(slot_tab[1, slot] > 0)
    def _():
        def visit(chunk, carry):
            devs = pl.ds(chunk * chunk_devs, chunk_devs)
            row = (lax.broadcasted_iota(jnp.int32, (chunk_rows, BLOCK), 0) + chunk * chunk_rows) // GRP
            ahead = lax.broadcasted_iota(jnp.int32, (chunk_rows, BLOCK), 1) - row
            visible = ahead <= offset
            wide = lax.broadcasted_iota(jnp.int32, (chunk_rows, HD), 1) % KVH
            before_lse = accl[previous, devs].reshape(chunk_rows, HD)
            packed = jnp.zeros((chunk_rows, HD), jnp.float32)
            for head in range(KVH):
                query = q_ref[devs, 0, head].astype(jnp.float32)
                query = query.reshape(chunk_rows, HD).astype(jnp.bfloat16)
                key = k_ref[:, head * HD : (head + 1) * HD]
                value = v_ref[:, head * HD : (head + 1) * HD]
                scores = lax.dot_general(
                    query, key, (((1,), (1,)), ((), ())), preferred_element_type=jnp.float32
                ) * (1.0 / math.sqrt(HD))
                scores = jnp.where(visible, scores, neg_big)
                highest = jnp.max(scores, axis=1, keepdims=True)
                weights = jnp.exp(scores - highest)
                total = jnp.sum(weights, axis=1, keepdims=True)
                weights = (weights * (1.0 / total)).astype(jnp.bfloat16)
                partial = jnp.dot(weights, value, preferred_element_type=jnp.float32)
                partial = partial.astype(jnp.bfloat16).astype(jnp.float32)
                lse = highest + jnp.log(total)
                old_lse = before_lse[:, head : head + 1]
                old = acc[previous, devs, head].astype(jnp.float32).reshape(chunk_rows, HD)
                peak = jnp.maximum(lse, old_lse)
                new_part = jnp.exp(lse - peak)
                old_part = jnp.exp(old_lse - peak)
                both = new_part + old_part
                scale = 1.0 / both
                partial = (new_part * scale) * partial + (old_part * scale) * old
                acc[slot, devs, head] = partial.reshape(chunk_devs, sub, HD).astype(jnp.bfloat16)
                packed = jnp.where(wide == head, peak + jnp.log(both), packed)
            accl[slot, devs] = packed.reshape(chunk_devs, sub, HD)
            return carry

        lax.fori_loop(0, chunks, visit, 0)


def scatter_kernel(
    cores,
    tiles,
    last_tab,
    acc,
    accl,
    out_ref,
    upbuf,
    dnbuf,
    psend,
    precv,
    xbuf,
    rs_up_out,
    rs_up,
    rs_dn_out,
    rs_dn,
    rs_pt_out,
    rs_pt,
):
    _, n_dev, _, sub, _ = acc.shape
    group = tiles // PIECES
    ring = Ring(n_dev, cores)
    chips, ups, dns, cores = ring.chips, ring.ups, ring.dns, ring.cores
    me, z, core = ring.me, ring.z, ring.core
    above, below, partner = ring.above, ring.below, ring.partner

    def drain(ref, sem):
        remote(ref, ref, sem, sem, partner).wait_recv()

    def gone(ref, sem):
        remote(ref, ref, sem, sem, partner).wait_send()

    ring.greet()
    lane = lax.broadcasted_iota(jnp.int32, (sub, HD), 1)
    lane_tile = lane // KVH

    def split_lse(value):
        parts = []
        rest = value
        for _ in range(TERMS):
            part = rest.astype(jnp.bfloat16)
            rest = rest - part.astype(jnp.float32)
            parts.append(part)
        return parts

    def store_lse(ref, value):
        for term, part in enumerate(split_lse(value)):
            ref[group * KVH + term] = part

    def read_lse(ref):
        total = ref[group * KVH].astype(jnp.float32)
        for term in range(1, TERMS):
            total = total + ref[group * KVH + term].astype(jnp.float32)
        return total

    empty_lse = jnp.full((sub, HD), neg_big, jnp.float32)
    for ref in (upbuf, dnbuf):
        for piece in range(PIECES):
            ref[0, piece, pl.ds(0, group * KVH)] = jnp.zeros((group * KVH, sub, HD), ref.dtype)
            store_lse(ref.at[0, piece], empty_lse)

    def own_lse(dest, piece):
        value = empty_lse
        for spot in range(group):
            latest = last_tab[piece * group + spot]
            value = jnp.where(lane_tile == spot, accl[latest, dest], value)
        return value

    def own_part(dest, piece, spot, head):
        return acc[last_tab[piece * group + spot], dest, head].astype(jnp.float32)

    def combine(values):
        peak = values[0]
        for value in values[1:]:
            peak = jnp.maximum(peak, value)
        shares = [jnp.exp(value - peak) for value in values]
        total = shares[0]
        for share in shares[1:]:
            total = total + share
        scale = 1.0 / total
        return [share * scale for share in shares], peak + jnp.log(total)

    def blend(refs, dest, piece, shares, spot, head):
        at = spot * KVH + head
        merged = shares[0][:, at : at + 1] * own_part(dest, piece, spot, head)
        for ref, share in zip(refs, shares[1:]):
            merged = merged + share[:, at : at + 1] * ref[at].astype(jnp.float32)
        return merged.astype(jnp.bfloat16)

    def give_partner(place, chip):
        dest = (chip % chips) * cores + (1 - core)
        for piece in range(PIECES):
            store_lse(psend.at[place, piece], own_lse(dest, piece))
            for spot in range(group):
                latest = last_tab[piece * group + spot]
                psend[place, piece, pl.ds(spot * KVH, KVH)] = acc[latest, dest]
        send(psend.at[place], precv.at[place], rs_pt_out.at[place], rs_pt.at[place], partner)

    def give_step(step):
        give_partner(step, z + ups - step)

        @pl.when(step < dns)
        def _():
            give_partner(ups + 1 + step, z + chips - dns + step)

    def hop(buf, step, place, chip, piece, out, recv, target):
        dest = (chip % chips) * cores + core

        @pl.when(step >= 1)
        def _():
            drain(buf.at[step, piece], recv.at[step - 1, piece])

        here = buf.at[step, piece]
        theirs = precv.at[place, piece]
        shares, lse = combine([own_lse(dest, piece), read_lse(here), read_lse(theirs)])
        for spot in range(group):
            for head in range(KVH):
                here[spot * KVH + head] = blend([here, theirs], dest, piece, shares, spot, head)
        store_lse(here, lse)
        send(here, buf.at[step + 1, piece], out.at[step, piece], recv.at[step, piece], target)

    give_step(0)

    def scatter_step(step, carry):
        @pl.when(step + 1 <= ups)
        def _():
            give_step(step + 1)

        drain(precv.at[step], rs_pt.at[step])

        @pl.when(step < dns)
        def _():
            drain(precv.at[ups + 1 + step], rs_pt.at[ups + 1 + step])

        for piece in range(PIECES):
            hop(upbuf, step, step, z + ups - step, piece, rs_up_out, rs_up, above)

            @pl.when(step < dns)
            def _():
                hop(
                    dnbuf,
                    step,
                    ups + 1 + step,
                    z + chips - dns + step,
                    piece,
                    rs_dn_out,
                    rs_dn,
                    below,
                )

        return carry

    lax.fori_loop(0, ups, scatter_step, 0)
    drain(precv.at[ups], rs_pt.at[ups])
    for piece in range(PIECES):
        drain(upbuf.at[ups, piece], rs_up.at[ups - 1, piece])
        drain(dnbuf.at[dns, piece], rs_dn.at[dns - 1, piece])
        refs = [upbuf.at[ups, piece], dnbuf.at[dns, piece], precv.at[ups, piece]]
        shares, _ = combine([own_lse(me, piece)] + [read_lse(ref) for ref in refs])
        for spot in range(group):
            for head in range(KVH):
                base = ((piece * group + spot) * KVH + head) * sub
                merged = blend(refs, me, piece, shares, spot, head)
                xbuf[pl.ds(base, sub)] = merged.astype(jnp.float32)
    for row in range(sub // GRP):
        for head in range(QH):
            first = (head // GRP) * sub + row * GRP + head % GRP
            picked = xbuf[pl.ds(first, tiles, stride=KVH * sub)]
            out_ref[pl.ds(row * tiles, tiles), head * HD : (head + 1) * HD] = picked.astype(
                jnp.bfloat16
            )

    def left(step, carry):
        for piece in range(PIECES):
            gone(upbuf.at[step, piece], rs_up_out.at[step, piece])

            @pl.when(step < dns)
            def _():
                gone(dnbuf.at[step, piece], rs_dn_out.at[step, piece])

        return carry

    lax.fori_loop(0, ups, left, 0)

    def left_partner(chip, carry):
        gone(psend.at[chip], rs_pt_out.at[chip])
        return carry

    lax.fori_loop(0, chips, left_partner, 0)


def on_device(cores, queries, keys, values, out_weight, chosen, tile_start):
    n_dev = lax.axis_size("blk")
    local_rows, tiles, width = queries.shape
    per_device = keys.shape[0] // BLOCK
    slots = per_device * CAP
    sub = local_rows * GRP
    chips = n_dev // cores
    ups = chips // 2
    dns = chips - 1 - ups
    slabs = tiles // PIECES * KVH + TERMS
    shards = queries.reshape(local_rows, tiles, KVH, GRP, HD)
    shards = jnp.transpose(shards, (1, 2, 0, 3, 4)).reshape(tiles, KVH, sub, HD)
    half = jnp.bfloat16
    wide = jnp.float32
    rings = [
        pltpu.SemaphoreType.DMA((ups, PIECES)),
        pltpu.SemaphoreType.DMA((ups, PIECES)),
        pltpu.SemaphoreType.DMA((dns, PIECES)),
        pltpu.SemaphoreType.DMA((dns, PIECES)),
        pltpu.SemaphoreType.DMA((chips,)),
        pltpu.SemaphoreType.DMA((chips,)),
    ]
    in_smem = pl.BlockSpec(memory_space=pltpu.SMEM)
    in_vmem = pl.BlockSpec(memory_space=pltpu.VMEM)
    anywhere = pl.BlockSpec(memory_space=pl.ANY)
    gathered_shape = (n_dev, tiles, KVH, sub, HD)
    gathered, slot_tab, last_tab = pl.pallas_call(
        functools.partial(gather_kernel, cores, per_device),
        out_shape=(
            jax.ShapeDtypeStruct(gathered_shape, half),
            jax.ShapeDtypeStruct((3, slots), jnp.int32),
            jax.ShapeDtypeStruct((tiles,), jnp.int32),
        ),
        in_specs=[in_smem, anywhere],
        out_specs=(anywhere, in_smem, in_smem),
        scratch_shapes=[
            pltpu.VMEM(gathered_shape, half),
            pltpu.SemaphoreType.DMA,
            pltpu.SemaphoreType.DMA((n_dev,)),
        ]
        + rings,
        compiler_params=pltpu.CompilerParams(
            collective_id=0, has_side_effects=True, vmem_limit_bytes=VMEM_LIMIT
        ),
        name="gather_queries",
    )(chosen, shards)
    acc_shape = (slots + 1, n_dev, KVH, sub, HD)
    accl_shape = (slots + 1, n_dev, sub, HD)
    acc, accl = pl.pallas_call(
        visit_kernel,
        out_shape=(
            jax.ShapeDtypeStruct(acc_shape, half),
            jax.ShapeDtypeStruct(accl_shape, wide),
        ),
        grid_spec=pltpu.PrefetchScalarGridSpec(
            num_scalar_prefetch=2,
            grid=(slots,),
            in_specs=[
                pl.BlockSpec((n_dev, 1, KVH, sub, HD), lambda s, tab, start: (0, tab[0, s], 0, 0, 0)),
                pl.BlockSpec((BLOCK, KVH * HD), lambda s, tab, start: (s // CAP, 0)),
                pl.BlockSpec((BLOCK, KVH * HD), lambda s, tab, start: (s // CAP, 0)),
            ],
            out_specs=[
                pl.BlockSpec(acc_shape, lambda s, tab, start: (0, 0, 0, 0, 0)),
                pl.BlockSpec(accl_shape, lambda s, tab, start: (0, 0, 0, 0)),
            ],
        ),
        compiler_params=pltpu.CompilerParams(
            dimension_semantics=("arbitrary",), vmem_limit_bytes=VMEM_LIMIT
        ),
        name="visits",
    )(slot_tab, tile_start, gathered, keys, values)
    merged = pl.pallas_call(
        functools.partial(scatter_kernel, cores, tiles),
        out_shape=jax.ShapeDtypeStruct((local_rows * tiles, width), half),
        in_specs=[in_smem, in_vmem, in_vmem],
        out_specs=in_vmem,
        scratch_shapes=[
            pltpu.VMEM((ups + 1, PIECES, slabs, sub, HD), half),
            pltpu.VMEM((dns + 1, PIECES, slabs, sub, HD), half),
            pltpu.VMEM((chips, PIECES, slabs, sub, HD), half),
            pltpu.VMEM((chips, PIECES, slabs, sub, HD), half),
            pltpu.VMEM((tiles * KVH * sub, HD), wide),
        ]
        + rings,
        compiler_params=pltpu.CompilerParams(
            collective_id=1, has_side_effects=True, vmem_limit_bytes=VMEM_LIMIT
        ),
        name="merge_partials",
    )(last_tab, acc, accl)
    result = jnp.dot(merged, out_weight, preferred_element_type=jnp.float32).astype(jnp.bfloat16)
    return result.reshape(local_rows, tiles, out_weight.shape[1])


def solution(mesh):
    placed = (
        P("blk", "groups", None),
        P(("groups", "blk"), None),
        P(("groups", "blk"), None),
        P(),
        P("groups", None),
        P("groups"),
    )
    return jax.shard_map(
        functools.partial(on_device, 2),
        mesh=mesh,
        in_specs=placed,
        out_specs=P("blk", "groups", None),
        check_vma=False,
    )
```

time: 730 us -> 222 us (0.30)
  waiting for transfers between devices: 526 us -> 0 us
  Pallas kernels: 0 us -> 213 us
  local copies, waits for them, and re-layouts: 94.1 us -> 1.68 us
  other arithmetic: 33.9 us -> 0 us
  matrix products: 28.4 us -> 5.67 us
  starting transfers between devices: 21.8 us -> 0 us
  between operations: 13.6 us -> 0.02 us
  loops' own time: 10.4 us -> 0 us
    all_to_all x2 -> x0, waiting for transfers between devices: 376 us -> none  [the longest x1 357 us: on_device(): lax.all_to_all(part_out, 'blk', split_axis=1, concat_axis=1, tiled=True)]
    pallas_call x0 -> x3, Pallas kernels: none -> 213 us  [the longest x1 90.2 us: on_device(): pl.pallas_call(functools.partial(gather_kernel, cores, per_device), out_s...]
    all_gather x1 -> x0, waiting for transfers between devices: 150 us -> none  [on_device(): gathered = lax.all_gather(queries, 'blk', axis=0, tiled=True)]
    dynamic_slice x56 -> x0, local copies, waits for them, and re-layouts: 34.1 us -> none  [the longest x32 20.5 us: on_device(): partials, log_slots = lax.map(one_slot, (slot_queries, begins, local_block))]
    dot_general x18 -> x0, matrix products: 22.8 us -> none  [the longest x8 9.57 us: visit_block(): jnp.einsum('kgrj,jkd->rkgd', weights, value_view, preferred_element_type=...]
    all_to_all x2 -> x0, starting transfers between devices: 21.8 us -> none  [the longest x1 14.5 us: on_device(): lax.all_to_all(peak_out, 'blk', split_axis=1, concat_axis=1, tiled=True)]
    mul x2 -> x0, local copies, waits for them, and re-layouts: 14.4 us -> none  [on_device(): factor[..., None]]
    mul x1 -> x0, other arithmetic: 11.7 us -> none  [on_device(): factor[..., None]]
  transfers between devices with their start and end apart: 3 -> 0, of which waited for: 3 -> 0; matrix products, arithmetic and copies ran while one was open for 4% -> 0% of each run, Pallas kernels for 0% -> 0%
where the time goes in v1:
time: 222 us; the launch traced here: 221 us
  Pallas kernels  213 us (96%)
  matrix products  5.67 us (3%)
    pallas_call x1, Pallas kernels, on_device(): pl.pallas_call(functools.partial(gather_kernel, cores, per_device), out_s...  90.2 us
    pallas_call x1, Pallas kernels, on_device(): pl.pallas_call(functools.partial(scatter_kernel, cores, tiles), out_shape...  88.6 us
    pallas_call x1, Pallas kernels, on_device(): pl.pallas_call(visit_kernel, out_shape=(jax.ShapeDtypeStruct(acc_shape, h...  34.7 us
    dot_general x1, matrix products, on_device(): jnp.dot(merged, out_weight, preferred_element_type=jnp.float32)  5.67 us

profile of v1, /device:TPU:46, one launch (start us, length us, event | category | flops | bytes accessed | tf_op | source)
XLA Modules:
  0.0 220.8 jit_solution(6316629534307790969)
XLA Ops:
  0.0 1.0 reshape.9
  1.0 0.7 copy.7
  1.7 90.2 %gather_queries.1 = (bf16[64,16,4,8,128]{4,3,2,1,0:T(8,128)(2,1)}, s32[3,8]{1,0:T(4,128)}, s32[16]{0:T(128)}) custom-call(s32[16,12]{1,0:T(8,128)} %chosen_ref.1, bf16[16,4,8,128]{3,2,1,0:T(8,128)(2,1)} %bitcast.6), custom_call_target="tpu_custom_call" | custom-call | tf_op jit(solution)/shard_map/gather_queries/pallas_call | solution.py:490
  91.9 34.7 %visits.1 = (bf16[9,64,4,8,128]{4,3,2,1,0:T(8,128)(2,1)}, f32[9,64,8,128]{3,2,1,0:T(8,128)}) custom-call(s32[3,8]{1,0:T(4,128)} %get-tuple-element.11.slot_tab, s32[16]{0:T(128)} %start_ref.1, bf16[64,16,4,8,128]{4,3,2,1,0:T(8,128)(2,1)} %get-tuple-element.12.q_ref, bf16[2048,512]{1,0:T(8,128)(2,1)} %k_ref.1, bf16[2048,512]{1,0:T(8,128)(2,1)} %v_ref.1), custom_call_target="tpu_custom_call" | custom-call | tf_op jit(solution)/shard_map/visits/pallas_call | solution.py:512
  126.6 88.6 %merge_partials.1 = bf16[32,2048]{1,0:T(8,128)(2,1)} custom-call(s32[16]{0:T(128)} %get-tuple-element.10.last_tab, bf16[9,64,4,8,128]{4,3,2,1,0:T(8,128)(2,1)} %get-tuple-element.13.acc, f32[9,64,8,128]{3,2,1,0:T(8,128)} %get-tuple-element.14.accl), custom_call_target="tpu_custom_call" | custom-call | tf_op jit(solution)/shard_map/merge_partials/pallas_call | solution.py:536
  215.2 5.7 %convolution_convert_fusion = bf16[32,2048]{1,0:T(8,128)(2,1)} fusion(bf16[32,2048]{1,0:T(8,128)(2,1)} %merge_partials.1, bf16[2048,2048]{1,0:T(8,128)(2,1)} %param.9), kind=kOutput, calls=%fused_computation | convolution fusion | flops 268500992 | bytes 8650752 | tf_op jit(solution)/shard_map/dot_general | solution.py:554

commit v2 on v1

--- a/solution.py
+++ b/solution.py
@@ -14,9 +14,9 @@
 HD = 128
 BLOCK = 512
 CAP = 2
-PIECES = 2
+PIECES = 4
 TERMS = 3
-CHUNK_ROWS = 128
+CHUNK_ROWS = 256
 VMEM_LIMIT = 60 * 1024 * 1024
 
 MESH = pl.DeviceIdType.MESH
@@ -230,11 +230,12 @@
 
     @pl.when(slot_tab[1, slot] > 0)
     def _():
-        def visit(chunk, carry):
+        def visit(chunk, masked):
             devs = pl.ds(chunk * chunk_devs, chunk_devs)
-            row = (lax.broadcasted_iota(jnp.int32, (chunk_rows, BLOCK), 0) + chunk * chunk_rows) // GRP
-            ahead = lax.broadcasted_iota(jnp.int32, (chunk_rows, BLOCK), 1) - row
-            visible = ahead <= offset
+            if masked:
+                row = lax.broadcasted_iota(jnp.int32, (chunk_rows, BLOCK), 0) + chunk * chunk_rows
+                ahead = lax.broadcasted_iota(jnp.int32, (chunk_rows, BLOCK), 1) - row // GRP
+                visible = ahead <= offset
             wide = lax.broadcasted_iota(jnp.int32, (chunk_rows, HD), 1) % KVH
             before_lse = accl[previous, devs].reshape(chunk_rows, HD)
             packed = jnp.zeros((chunk_rows, HD), jnp.float32)
@@ -245,15 +246,16 @@
                 value = v_ref[:, head * HD : (head + 1) * HD]
                 scores = lax.dot_general(
                     query, key, (((1,), (1,)), ((), ())), preferred_element_type=jnp.float32
-                ) * (1.0 / math.sqrt(HD))
-                scores = jnp.where(visible, scores, neg_big)
+                )
+                if masked:
+                    scores = jnp.where(visible, scores, neg_big)
                 highest = jnp.max(scores, axis=1, keepdims=True)
-                weights = jnp.exp(scores - highest)
+                weights = jnp.exp2((scores - highest) * (math.log2(math.e) / math.sqrt(HD)))
                 total = jnp.sum(weights, axis=1, keepdims=True)
                 weights = (weights * (1.0 / total)).astype(jnp.bfloat16)
                 partial = jnp.dot(weights, value, preferred_element_type=jnp.float32)
                 partial = partial.astype(jnp.bfloat16).astype(jnp.float32)
-                lse = highest + jnp.log(total)
+                lse = highest * (1.0 / math.sqrt(HD)) + jnp.log(total)
                 old_lse = before_lse[:, head : head + 1]
                 old = acc[previous, devs, head].astype(jnp.float32).reshape(chunk_rows, HD)
                 peak = jnp.maximum(lse, old_lse)
@@ -265,9 +267,16 @@
                 acc[slot, devs, head] = partial.reshape(chunk_devs, sub, HD).astype(jnp.bfloat16)
                 packed = jnp.where(wide == head, peak + jnp.log(both), packed)
             accl[slot, devs] = packed.reshape(chunk_devs, sub, HD)
-            return carry
-
-        lax.fori_loop(0, chunks, visit, 0)
+
+        def visits(masked):
+            def step(chunk, carry):
+                visit(chunk, masked)
+                return carry
+
+            lax.fori_loop(0, chunks, step, 0)
+
+        pl.when(offset >= BLOCK - 1)(lambda: visits(False))
+        pl.when(offset < BLOCK - 1)(lambda: visits(True))
 
 
 def scatter_kernel(
@@ -304,25 +313,24 @@
 
     ring.greet()
     lane = lax.broadcasted_iota(jnp.int32, (sub, HD), 1)
-    lane_tile = lane // KVH
-
-    def split_lse(value):
-        parts = []
+    width = group * KVH
+    lane_tile = (lane % width) // KVH
+
+    def store_lse(ref, value):
+        packed = jnp.zeros_like(value)
         rest = value
-        for _ in range(TERMS):
-            part = rest.astype(jnp.bfloat16)
-            rest = rest - part.astype(jnp.float32)
-            parts.append(part)
-        return parts
-
-    def store_lse(ref, value):
-        for term, part in enumerate(split_lse(value)):
-            ref[group * KVH + term] = part
+        for term in range(TERMS):
+            part = rest.astype(jnp.bfloat16).astype(jnp.float32)
+            rest = rest - part
+            here = (lane >= term * width) & (lane < (term + 1) * width)
+            packed = jnp.where(here, pltpu.roll(part, term * width, 1) if term else part, packed)
+        ref[group * KVH] = packed.astype(jnp.bfloat16)
 
     def read_lse(ref):
-        total = ref[group * KVH].astype(jnp.float32)
+        packed = ref[group * KVH].astype(jnp.float32)
+        total = packed
         for term in range(1, TERMS):
-            total = total + ref[group * KVH + term].astype(jnp.float32)
+            total = total + pltpu.roll(packed, HD - term * width, 1)
         return total
 
     empty_lse = jnp.full((sub, HD), neg_big, jnp.float32)
@@ -470,7 +478,7 @@
     chips = n_dev // cores
     ups = chips // 2
     dns = chips - 1 - ups
-    slabs = tiles // PIECES * KVH + TERMS
+    slabs = tiles // PIECES * KVH + 1
     shards = queries.reshape(local_rows, tiles, KVH, GRP, HD)
     shards = jnp.transpose(shards, (1, 2, 0, 3, 4)).reshape(tiles, KVH, sub, HD)
     half = jnp.bfloat16

time: 222 us -> 197 us (0.89)
  Pallas kernels: 213 us -> 188 us
    pallas_call x1, Pallas kernels: 88.6 us -> 71.8 us  [on_device(): pl.pallas_call(functools.partial(scatter_kernel, cores, tiles), out_shape...]
    pallas_call x1, Pallas kernels: 34.7 us -> 30.1 us  [on_device(): pl.pallas_call(visit_kernel, out_shape=(jax.ShapeDtypeStruct(acc_shape, h...]
    pallas_call x1, Pallas kernels: 90.2 us -> 86 us  [on_device(): pl.pallas_call(functools.partial(gather_kernel, cores, per_device), out_s...]
where the time goes in v2:
time: 197 us; the launch traced here: 195 us
  Pallas kernels  188 us (95%)
  matrix products  5.67 us (3%)
    pallas_call x1, Pallas kernels, on_device(): pl.pallas_call(functools.partial(gather_kernel, cores, per_device), out_s...  86 us
    pallas_call x1, Pallas kernels, on_device(): pl.pallas_call(functools.partial(scatter_kernel, cores, tiles), out_shape...  71.8 us
    pallas_call x1, Pallas kernels, on_device(): pl.pallas_call(visit_kernel, out_shape=(jax.ShapeDtypeStruct(acc_shape, h...  30.1 us
    dot_general x1, matrix products, on_device(): jnp.dot(merged, out_weight, preferred_element_type=jnp.float32)  5.67 us

profile of v2, /device:TPU:46, one launch (start us, length us, event | category | flops | bytes accessed | tf_op | source)
XLA Modules:
  0.0 195.2 jit_solution(16036120400346054858)
XLA Ops:
  0.0 1.0 reshape.9
  1.0 0.7 copy.7
  1.7 86.0 %gather_queries.1 = (bf16[64,16,4,8,128]{4,3,2,1,0:T(8,128)(2,1)}, s32[3,8]{1,0:T(4,128)}, s32[16]{0:T(128)}) custom-call(s32[16,12]{1,0:T(8,128)} %chosen_ref.1, bf16[16,4,8,128]{3,2,1,0:T(8,128)(2,1)} %bitcast.6), custom_call_target="tpu_custom_call" | custom-call | tf_op jit(solution)/shard_map/gather_queries/pallas_call | solution.py:498
  87.7 30.1 %visits.1 = (bf16[9,64,4,8,128]{4,3,2,1,0:T(8,128)(2,1)}, f32[9,64,8,128]{3,2,1,0:T(8,128)}) custom-call(s32[3,8]{1,0:T(4,128)} %get-tuple-element.11.slot_tab, s32[16]{0:T(128)} %start_ref.1, bf16[64,16,4,8,128]{4,3,2,1,0:T(8,128)(2,1)} %get-tuple-element.12.q_ref, bf16[2048,512]{1,0:T(8,128)(2,1)} %k_ref.1, bf16[2048,512]{1,0:T(8,128)(2,1)} %v_ref.1), custom_call_target="tpu_custom_call" | custom-call | tf_op jit(solution)/shard_map/visits/pallas_call | solution.py:520
  117.7 71.8 %merge_partials.1 = bf16[32,2048]{1,0:T(8,128)(2,1)} custom-call(s32[16]{0:T(128)} %get-tuple-element.10.last_tab, bf16[9,64,4,8,128]{4,3,2,1,0:T(8,128)(2,1)} %get-tuple-element.13.acc, f32[9,64,8,128]{3,2,1,0:T(8,128)} %get-tuple-element.14.accl), custom_call_target="tpu_custom_call" | custom-call | tf_op jit(solution)/shard_map/merge_partials/pallas_call | solution.py:544
  189.5 5.7 %convolution_convert_fusion = bf16[32,2048]{1,0:T(8,128)(2,1)} fusion(bf16[32,2048]{1,0:T(8,128)(2,1)} %merge_partials.1, bf16[2048,2048]{1,0:T(8,128)(2,1)} %param.9), kind=kOutput, calls=%fused_computation | convolution fusion | flops 268500992 | bytes 8650752 | tf_op jit(solution)/shard_map/dot_general | solution.py:562

commit v3 on v2

--- a/solution.py
+++ b/solution.py
@@ -15,6 +15,7 @@
 BLOCK = 512
 CAP = 2
 PIECES = 4
+SHARD_PIECES = 8
 TERMS = 3
 CHUNK_ROWS = 256
 VMEM_LIMIT = 60 * 1024 * 1024
@@ -77,7 +78,7 @@
 ):
     n_dev, tiles, _, sub, _ = gath.shape
     slots = per_device * CAP
-    group = tiles // PIECES
+    group = tiles // SHARD_PIECES
     topk = chosen_ref.shape[1]
     ring = Ring(n_dev, cores)
     chips, ups, dns, cores = ring.chips, ring.ups, ring.dns, ring.cores
@@ -101,11 +102,12 @@
     def to_partner(index):
         part = gath.at[index]
         send(part, part, ag_pt_out.at[index // cores], ag_pt.at[index // cores], partner)
+        pltpu.make_async_copy(part, all_hbm.at[index], store_sem.at[index]).start()
 
     def gather_step(step, carry):
         from_below = ((z - step + chips) % chips) * cores + core
         from_above = ((z + step) % chips) * cores + core
-        for piece in range(PIECES):
+        for piece in range(SHARD_PIECES):
             part = shard(from_below, piece)
 
             @pl.when(step >= 1)
@@ -170,22 +172,22 @@
 
     from_below = ((z - ups + chips) % chips) * cores + core
     from_above = ((z + dns) % chips) * cores + core
-    for piece in range(PIECES):
+    for piece in range(SHARD_PIECES):
         drain(shard(from_below, piece), ag_up.at[ups - 1, piece])
     to_partner(from_below)
-    for piece in range(PIECES):
+    for piece in range(SHARD_PIECES):
         drain(shard(from_above, piece), ag_dn.at[dns - 1, piece])
     to_partner(from_above)
 
     def partner_shard(chip, carry):
         drain(gath.at[chip * cores + (1 - core)], ag_pt.at[chip])
-        for index in (chip * cores + core, chip * cores + (1 - core)):
-            pltpu.make_async_copy(gath.at[index], all_hbm.at[index], store_sem.at[index]).start()
+        index = chip * cores + (1 - core)
+        pltpu.make_async_copy(gath.at[index], all_hbm.at[index], store_sem.at[index]).start()
         return carry
 
     lax.fori_loop(0, chips, partner_shard, 0)
     def left(step, carry):
-        for piece in range(PIECES):
+        for piece in range(SHARD_PIECES):
             gone(shard(((z - step + chips) % chips) * cores + core, piece), ag_up_out.at[step, piece])
 
             @pl.when(step < dns)
@@ -239,6 +241,8 @@
             wide = lax.broadcasted_iota(jnp.int32, (chunk_rows, HD), 1) % KVH
             before_lse = accl[previous, devs].reshape(chunk_rows, HD)
             packed = jnp.zeros((chunk_rows, HD), jnp.float32)
+            olds = [acc[previous, devs, head] for head in range(KVH)]
+            partials = []
             for head in range(KVH):
                 query = q_ref[devs, 0, head].astype(jnp.float32)
                 query = query.reshape(chunk_rows, HD).astype(jnp.bfloat16)
@@ -257,15 +261,17 @@
                 partial = partial.astype(jnp.bfloat16).astype(jnp.float32)
                 lse = highest * (1.0 / math.sqrt(HD)) + jnp.log(total)
                 old_lse = before_lse[:, head : head + 1]
-                old = acc[previous, devs, head].astype(jnp.float32).reshape(chunk_rows, HD)
+                old = olds[head].astype(jnp.float32).reshape(chunk_rows, HD)
                 peak = jnp.maximum(lse, old_lse)
                 new_part = jnp.exp(lse - peak)
                 old_part = jnp.exp(old_lse - peak)
                 both = new_part + old_part
                 scale = 1.0 / both
                 partial = (new_part * scale) * partial + (old_part * scale) * old
-                acc[slot, devs, head] = partial.reshape(chunk_devs, sub, HD).astype(jnp.bfloat16)
+                partials.append(partial.reshape(chunk_devs, sub, HD).astype(jnp.bfloat16))
                 packed = jnp.where(wide == head, peak + jnp.log(both), packed)
+            for head in range(KVH):
+                acc[slot, devs, head] = partials[head]
             accl[slot, devs] = packed.reshape(chunk_devs, sub, HD)
 
         def visits(masked):
@@ -365,7 +371,7 @@
         merged = shares[0][:, at : at + 1] * own_part(dest, piece, spot, head)
         for ref, share in zip(refs, shares[1:]):
             merged = merged + share[:, at : at + 1] * ref[at].astype(jnp.float32)
-        return merged.astype(jnp.bfloat16)
+        return merged
 
     def give_partner(place, chip):
         dest = (chip % chips) * cores + (1 - core)
@@ -386,16 +392,23 @@
     def hop(buf, step, place, chip, piece, out, recv, target):
         dest = (chip % chips) * cores + core
 
+        here = buf.at[step, piece]
+        theirs = precv.at[place, piece]
+        local, local_lse = combine([own_lse(dest, piece), read_lse(theirs)])
+        parts = [
+            blend([theirs], dest, piece, local, spot, head)
+            for spot in range(group)
+            for head in range(KVH)
+        ]
+
         @pl.when(step >= 1)
         def _():
-            drain(buf.at[step, piece], recv.at[step - 1, piece])
-
-        here = buf.at[step, piece]
-        theirs = precv.at[place, piece]
-        shares, lse = combine([own_lse(dest, piece), read_lse(here), read_lse(theirs)])
-        for spot in range(group):
-            for head in range(KVH):
-                here[spot * KVH + head] = blend([here, theirs], dest, piece, shares, spot, head)
+            drain(here, recv.at[step - 1, piece])
+
+        shares, lse = combine([local_lse, read_lse(here)])
+        for at, part in enumerate(parts):
+            arrived = shares[1][:, at : at + 1] * here[at].astype(jnp.float32)
+            here[at] = (shares[0][:, at : at + 1] * part + arrived).astype(jnp.bfloat16)
         store_lse(here, lse)
         send(here, buf.at[step + 1, piece], out.at[step, piece], recv.at[step, piece], target)
 
@@ -441,7 +454,7 @@
             for head in range(KVH):
                 base = ((piece * group + spot) * KVH + head) * sub
                 merged = blend(refs, me, piece, shares, spot, head)
-                xbuf[pl.ds(base, sub)] = merged.astype(jnp.float32)
+                xbuf[pl.ds(base, sub)] = merged.astype(jnp.bfloat16).astype(jnp.float32)
     for row in range(sub // GRP):
         for head in range(QH):
             first = (head // GRP) * sub + row * GRP + head % GRP
@@ -483,14 +496,17 @@
     shards = jnp.transpose(shards, (1, 2, 0, 3, 4)).reshape(tiles, KVH, sub, HD)
     half = jnp.bfloat16
     wide = jnp.float32
-    rings = [
-        pltpu.SemaphoreType.DMA((ups, PIECES)),
-        pltpu.SemaphoreType.DMA((ups, PIECES)),
-        pltpu.SemaphoreType.DMA((dns, PIECES)),
-        pltpu.SemaphoreType.DMA((dns, PIECES)),
-        pltpu.SemaphoreType.DMA((chips,)),
-        pltpu.SemaphoreType.DMA((chips,)),
-    ]
+
+    def rings(pieces):
+        return [
+            pltpu.SemaphoreType.DMA((ups, pieces)),
+            pltpu.SemaphoreType.DMA((ups, pieces)),
+            pltpu.SemaphoreType.DMA((dns, pieces)),
+            pltpu.SemaphoreType.DMA((dns, pieces)),
+            pltpu.SemaphoreType.DMA((chips,)),
+            pltpu.SemaphoreType.DMA((chips,)),
+        ]
+
     in_smem = pl.BlockSpec(memory_space=pltpu.SMEM)
     in_vmem = pl.BlockSpec(memory_space=pltpu.VMEM)
     anywhere = pl.BlockSpec(memory_space=pl.ANY)
@@ -509,7 +525,7 @@
             pltpu.SemaphoreType.DMA,
             pltpu.SemaphoreType.DMA((n_dev,)),
         ]
-        + rings,
+        + rings(SHARD_PIECES),
         compiler_params=pltpu.CompilerParams(
             collective_id=0, has_side_effects=True, vmem_limit_bytes=VMEM_LIMIT
         ),
@@ -553,7 +569,7 @@
             pltpu.VMEM((chips, PIECES, slabs, sub, HD), half),
             pltpu.VMEM((tiles * KVH * sub, HD), wide),
         ]
-        + rings,
+        + rings(PIECES),
         compiler_params=pltpu.CompilerParams(
             collective_id=1, has_side_effects=True, vmem_limit_bytes=VMEM_LIMIT
         ),

time: 197 us -> 197 us (level)
    pallas_call x1, Pallas kernels: 30.1 us -> 22.9 us  [on_device(): pl.pallas_call(visit_kernel, out_shape=(jax.ShapeDtypeStruct(acc_shape, h...]
    pallas_call x1, Pallas kernels: 71.8 us -> 78.7 us  [on_device(): pl.pallas_call(functools.partial(scatter_kernel, cores, tiles), out_shape...]
where the time goes in v3:
time: 197 us; the launch traced here: 194 us
  Pallas kernels  187 us (95%)
  matrix products  5.67 us (3%)
    pallas_call x1, Pallas kernels, on_device(): pl.pallas_call(functools.partial(gather_kernel, cores, per_device), out_s...  85.1 us
    pallas_call x1, Pallas kernels, on_device(): pl.pallas_call(functools.partial(scatter_kernel, cores, tiles), out_shape...  78.7 us
    pallas_call x1, Pallas kernels, on_device(): pl.pallas_call(visit_kernel, out_shape=(jax.ShapeDtypeStruct(acc_shape, h...  22.9 us
    dot_general x1, matrix products, on_device(): jnp.dot(merged, out_weight, preferred_element_type=jnp.float32)  5.67 us

profile of v3, /device:TPU:46, one launch (start us, length us, event | category | flops | bytes accessed | tf_op | source)
XLA Modules:
  0.0 194.1 jit_solution(637697068243529949)
XLA Ops:
  0.0 1.0 reshape.9
  1.0 0.7 copy.7
  1.7 85.1 %gather_queries.1 = (bf16[64,16,4,8,128]{4,3,2,1,0:T(8,128)(2,1)}, s32[3,8]{1,0:T(4,128)}, s32[16]{0:T(128)}) custom-call(s32[16,12]{1,0:T(8,128)} %chosen_ref.1, bf16[16,4,8,128]{3,2,1,0:T(8,128)(2,1)} %bitcast.6), custom_call_target="tpu_custom_call" | custom-call | tf_op jit(solution)/shard_map/gather_queries/pallas_call | solution.py:514
  86.8 22.9 %visits.1 = (bf16[9,64,4,8,128]{4,3,2,1,0:T(8,128)(2,1)}, f32[9,64,8,128]{3,2,1,0:T(8,128)}) custom-call(s32[3,8]{1,0:T(4,128)} %get-tuple-element.11.slot_tab, s32[16]{0:T(128)} %start_ref.1, bf16[64,16,4,8,128]{4,3,2,1,0:T(8,128)(2,1)} %get-tuple-element.12.q_ref, bf16[2048,512]{1,0:T(8,128)(2,1)} %k_ref.1, bf16[2048,512]{1,0:T(8,128)(2,1)} %v_ref.1), custom_call_target="tpu_custom_call" | custom-call | tf_op jit(solution)/shard_map/visits/pallas_call | solution.py:536
  109.7 78.7 %merge_partials.1 = bf16[32,2048]{1,0:T(8,128)(2,1)} custom-call(s32[16]{0:T(128)} %get-tuple-element.10.last_tab, bf16[9,64,4,8,128]{4,3,2,1,0:T(8,128)(2,1)} %get-tuple-element.13.acc, f32[9,64,8,128]{3,2,1,0:T(8,128)} %get-tuple-element.14.accl), custom_call_target="tpu_custom_call" | custom-call | tf_op jit(solution)/shard_map/merge_partials/pallas_call | solution.py:560
  188.4 5.7 %convolution_convert_fusion = bf16[32,2048]{1,0:T(8,128)(2,1)} fusion(bf16[32,2048]{1,0:T(8,128)(2,1)} %merge_partials.1, bf16[2048,2048]{1,0:T(8,128)(2,1)} %param.9), kind=kOutput, calls=%fused_computation | convolution fusion | flops 268500992 | bytes 8650752 | tf_op jit(solution)/shard_map/dot_general | solution.py:578
